TPU v7x, 32 devices: a whole 2x2x4 slice. The times are simulated.
32 devices in a mesh: row: 4 (over y, core), col: 8 (over z, x).
Axes of the slice: x: 2, y: 2, z: 4, core: 2. Of those that a mesh axis runs over, the one named last changes fastest.
Arguments:
- matrix: float32 [16384, 16384], P('row', 'col'), may hold values from -500 to 500
Outputs:
- reduced: float32 [16384, 16384], P('row', 'col')
All inputs are finite; a program needn't handle non-finite values.
Results may differ from a plain program's by a relative error of at most 0.0003.
Values sent between devices are 32-bit elements; how exact they have to be, the bound alone decides.
No kernel may reach another device: no remote copies, remote signals or barrier semaphores. Data moves between devices by JAX's collectives and lax.ppermute only.
A program may use at most 192 MiB of HBM per device.

v0:
```python
import jax
import jax.numpy as jnp
from jax import lax
from jax.sharding import PartitionSpec as P

REFL = 4
PANELS = 2


highest = lax.Precision.HIGHEST


def from_root(value, axis, source):
    kept = jnp.where(lax.axis_index(axis) == source, value, 0).astype(value.dtype)
    return lax.psum(kept, axis)


def product(left, right):
    return jnp.dot(left, right, precision=highest, preferred_element_type=jnp.float32)


def on_device(matrix):
    rows_local, cols_local = matrix.shape
    row_start = lax.axis_index("row") * rows_local
    col_start = lax.axis_index("col") * cols_local
    total = rows_local * lax.axis_size("row")
    positions = jnp.arange(total, dtype=jnp.int32)
    current = matrix
    for panel_index in range(PANELS):
        reflectors = jnp.zeros((total, REFL), jnp.float32)
        updates = jnp.zeros((total, REFL), jnp.float32)
        for inner_index in range(REFL):
            target = panel_index * REFL + inner_index
            owner = target // cols_local
            own_slice = current[:, target - owner * cols_local]
            reflector_rows = lax.dynamic_slice_in_dim(reflectors, row_start, rows_local, 0)
            update_block = lax.dynamic_slice_in_dim(updates, row_start, rows_local, 0)
            held = from_root(own_slice, "col", owner)
            column = (
                held
                - product(reflector_rows, updates[target])
                - product(update_block, reflectors[target])
            )
            whole = lax.all_gather(column, "row", axis=0, tiled=True)
            beneath = jnp.where(positions > target, whole, 0.0)
            leading = whole[target + 1]
            length = jnp.sqrt(jnp.sum(beneath * beneath))
            signed = jnp.where(leading >= 0.0, length, -length)
            vector = beneath + jnp.where(positions == target + 1, signed, 0.0)
            factor = 1.0 / (length * (length + jnp.abs(leading)))
            vector_cols = lax.dynamic_slice_in_dim(vector, col_start, cols_local, 0)
            against_updates = product(vector, updates)
            against_reflectors = product(vector, reflectors)
            summed = lax.psum(product(current, vector_cols), "col")
            mapped = factor * (
                summed
                - product(reflector_rows, against_updates)
                - product(update_block, against_reflectors)
            )
            vector_rows = lax.dynamic_slice_in_dim(vector, row_start, rows_local, 0)
            inner = lax.psum(jnp.sum(mapped * vector_rows), "row")
            update = lax.all_gather(
                mapped - 0.5 * factor * inner * vector_rows, "row", axis=0, tiled=True
            )
            reflectors = reflectors.at[:, inner_index].set(vector)
            updates = updates.at[:, inner_index].set(update)
        reflector_rows = lax.dynamic_slice_in_dim(reflectors, row_start, rows_local, 0)
        update_block = lax.dynamic_slice_in_dim(updates, row_start, rows_local, 0)
        reflector_cols = lax.dynamic_slice_in_dim(reflectors, col_start, cols_local, 0)
        update_cols = lax.dynamic_slice_in_dim(updates, col_start, cols_local, 0)
        current = (
            current
            - product(reflector_rows, update_cols.T)
            - product(update_block, reflector_cols.T)
        )
    return current


def solution(mesh):
    return jax.shard_map(
        on_device,
        mesh=mesh,
        in_specs=(P("row", "col"),),
        out_specs=P("row", "col"),
        check_vma=False,
    )
```

profile of v0, /device:TPU:0, one launch (start us, length us, event | category | flops | bytes accessed | tf_op | source)
XLA Modules:
  0.0 982.2 jit_solution(17959320532915637002)
XLA Ops:
  3.4 31.1 %copy.46 = f32[4096,2048]{0,1:T(8,128)} copy(f32[4096,2048]{1,0:T(8,128)} %param.33) | data formatting | bytes 67108864 | tf_op args[0]
  34.5 1.3 broadcast_select_fusion.16
  35.8 38.8 %psum.168 = f32[4096]{0:T(1024)S(1)} all-reduce(f32[4096]{0:T(1024)S(1)} %bitcast.324), channel_id=1, replica_groups=mesh['row'=4,'col'=8] {'col'}, use_global_device_ids=true, to_apply=%region_1.2 | all-reduce | flops 4096 | bytes 32768 | tf_op jit(solution)/shard_map/psum | solution.py:15
  74.7 5.2 all_gather.48
  83.8 1.9 fusion.2
  85.9 30.7 %fusion.128 = f32[1,4096]{1,0:T(1,128)S(1)} fusion(f32[2048,1]{0,1:T(1,128)S(1)} %bitcast.325, f32[4096,2048]{1,0:T(8,128)} %param.33), kind=kOutput, calls=%fused_computation.249 | convolution fusion | flops 100663296 | bytes 33579008 | tf_op jit(solution)/shard_map/dot_general | solution.py:19
  116.6 33.1 %all-reduce.9 = (f32[4096]{0:T(1024)S(1)}, f32[4096]{0:T(1024)S(1)}) all-reduce(f32[4096]{0:T(1024)S(1)} %bitcast.289, f32[4096]{0:T(1024)S(1)} %bitcast.322), channel_id=1, replica_groups=mesh['row'=4,'col'=8] {'col'}, use_global_device_ids=true, to_apply=%region_5.6 | all-reduce | flops 8192 | bytes 65536 | tf_op jit(solution)/shard_map/psum | solution.py:54
  151.1 6.3 psum.171
  158.1 5.2 all_gather.49
  164.8 5.5 all_gather.50
  174.2 1.3 convolution_bitcast_fusion.11
  175.5 1.3 convolution_bitcast_fusion.12
  176.8 30.7 %fusion.129 = f32[1,4096]{1,0:T(1,128)S(1)} fusion(f32[2048,1]{0,1:T(1,128)S(1)} %bitcast.326, f32[4096,2048]{1,0:T(8,128)} %param.33), kind=kOutput, calls=%fused_computation.250 | convolution fusion | flops 100663296 | bytes 33579008 | tf_op jit(solution)/shard_map/dot_general | solution.py:19
  207.5 33.1 %all-reduce.8 = (f32[4096]{0:T(1024)S(1)}, f32[4096]{0:T(1024)S(1)}) all-reduce(f32[4096]{0:T(1024)S(1)} %bitcast.290, f32[4096]{0:T(1024)S(1)} %bitcast.320), channel_id=1, replica_groups=mesh['row'=4,'col'=8] {'col'}, use_global_device_ids=true, to_apply=%region_11.12 | all-reduce | flops 8192 | bytes 65536 | tf_op jit(solution)/shard_map/psum | solution.py:54
  241.8 6.3 psum.174
  248.6 5.2 all_gather.51
  257.9 5.7 all_gather.52
  266.9 1.3 convolution_bitcast_fusion.9
  268.2 1.3 convolution_bitcast_fusion.10
  269.5 30.7 %fusion.130 = f32[1,4096]{1,0:T(1,128)S(1)} fusion(f32[2048,1]{0,1:T(1,128)S(1)} %bitcast.327, f32[4096,2048]{1,0:T(8,128)} %param.33), kind=kOutput, calls=%fused_computation.251 | convolution fusion | flops 100663296 | bytes 33579008 | tf_op jit(solution)/shard_map/dot_general | solution.py:19
  300.2 33.1 %all-reduce.7 = (f32[4096]{0:T(1024)S(1)}, f32[4096]{0:T(1024)S(1)}) all-reduce(f32[4096]{0:T(1024)S(1)} %bitcast.291, f32[4096]{0:T(1024)S(1)} %bitcast.318), channel_id=1, replica_groups=mesh['row'=4,'col'=8] {'col'}, use_global_device_ids=true, to_apply=%region_16.17 | all-reduce | flops 8192 | bytes 65536 | tf_op jit(solution)/shard_map/psum | solution.py:54
  334.5 6.3 psum.177
  341.3 5.2 all_gather.53
  351.4 5.5 all_gather.54
  360.2 1.3 convolution_bitcast_fusion.7
  361.5 1.3 convolution_bitcast_fusion.8
  362.8 30.7 %fusion.131 = f32[1,4096]{1,0:T(1,128)S(1)} fusion(f32[2048,1]{0,1:T(1,128)S(1)} %bitcast.328, f32[4096,2048]{1,0:T(8,128)} %param.33), kind=kOutput, calls=%fused_computation.252 | convolution fusion | flops 100663296 | bytes 33579008 | tf_op jit(solution)/shard_map/dot_general | solution.py:19
  393.5 33.0 %psum.178 = f32[4096]{0:T(1024)S(1)} all-reduce(f32[4096]{0:T(1024)S(1)} %bitcast.292), channel_id=1, replica_groups=mesh['row'=4,'col'=8] {'col'}, use_global_device_ids=true, to_apply=%region_20.21 | all-reduce | flops 4096 | bytes 32768 | tf_op jit(solution)/shard_map/psum | solution.py:54
  428.9 6.3 psum.179
  435.7 5.4 all_gather.55
  442.3 30.1 %fusion.14 = f32[4096,2048]{0,1:T(8,128)} fusion(f32[16384,4]{0,1:T(4,128)S(1)} %scatter.64, s32[]{:T(128)S(6)} %select_n.183, f32[16384,4]{0,1:T(4,128)S(1)} %scatter.65, s32[]{:T(128)S(6)} %select_n.184), kind=kOutput, calls=%fused_computation.58 | convolution fusion | flops 402653184 | bytes 33652744 | tf_op jit(solution)/shard_map/dot_general | solution.py:19
  472.4 41.2 %subtract_subtract_fusion.1 = f32[4096,2048]{0,1:T(8,128)} fusion(f32[4096,2048]{0,1:T(8,128)} %copy.46, f32[4096,2048]{0,1:T(8,128)} %fusion.14, f32[16384,4]{0,1:T(4,128)S(1)} %scatter.65, s32[]{:T(128)S(6)} %select_n.183, f32[16384,4]{0,1:T(4,128)S(1)} %scatter.64, s32[]{:T(128)S(6)} %select_n.184), kind=kOutput, calls=%fused_computation.1 | convolution fusion | flops 419430400 | bytes 100761608 | tf_op jit(solution)/shard_map/dot_general | solution.py:19
  513.7 1.3 broadcast_select_fusion.12
  515.0 33.0 %psum.180 = f32[4096]{0:T(1024)S(1)} all-reduce(f32[4096]{0:T(1024)S(1)} %bitcast.323), channel_id=1, replica_groups=mesh['row'=4,'col'=8] {'col'}, use_global_device_ids=true, to_apply=%region_23.24 | all-reduce | flops 4096 | bytes 32768 | tf_op jit(solution)/shard_map/psum | solution.py:15
  548.0 5.2 all_gather.56
  557.1 1.9 fusion.3
  559.2 21.5 %fusion.132 = f32[1,4096]{1,0:T(1,128)S(1)} fusion(f32[4096,2048]{0,1:T(8,128)} %subtract_subtract_fusion.1, f32[2048,1]{0,1:T(1,128)S(1)} %bitcast.329), kind=kOutput, calls=%fused_computation.253 | convolution fusion | flops 100663296 | bytes 33579008 | tf_op jit(solution)/shard_map/dot_general | solution.py:19
  580.7 33.1 %all-reduce.6 = (f32[4096]{0:T(1024)S(1)}, f32[4096]{0:T(1024)S(1)}) all-reduce(f32[4096]{0:T(1024)S(1)} %bitcast.285, f32[4096]{0:T(1024)S(1)} %bitcast.321), channel_id=1, replica_groups=mesh['row'=4,'col'=8] {'col'}, use_global_device_ids=true, to_apply=%region_26.27 | all-reduce | flops 8192 | bytes 65536 | tf_op jit(solution)/shard_map/psum | solution.py:54
  615.2 6.3 psum.183
  622.2 5.2 all_gather.57
  628.9 5.4 all_gather.58
  638.2 1.3 convolution_bitcast_fusion.4
  639.5 1.3 convolution_bitcast_fusion.5
  640.8 21.0 %fusion.133 = f32[1,4096]{1,0:T(1,128)S(1)} fusion(f32[4096,2048]{0,1:T(8,128)} %subtract_subtract_fusion.1, f32[2048,1]{0,1:T(1,128)S(1)} %bitcast.330), kind=kOutput, calls=%fused_computation.254 | convolution fusion | flops 100663296 | bytes 33579008 | tf_op jit(solution)/shard_map/dot_general | solution.py:19
  661.9 33.2 %all-reduce.5 = (f32[4096]{0:T(1024)S(1)}, f32[4096]{0:T(1024)S(1)}) all-reduce(f32[4096]{0:T(1024)S(1)} %bitcast.286, f32[4096]{0:T(1024)S(1)} %bitcast.319), channel_id=1, replica_groups=mesh['row'=4,'col'=8] {'col'}, use_global_device_ids=true, to_apply=%region_31.32 | all-reduce | flops 8192 | bytes 65536 | tf_op jit(solution)/shard_map/psum | solution.py:54
  696.3 6.3 psum.186
  703.2 5.2 all_gather.59
  712.4 5.3 all_gather.60
  721.0 1.3 convolution_bitcast_fusion.2
  722.3 1.3 convolution_bitcast_fusion.3
  723.6 21.0 %fusion.134 = f32[1,4096]{1,0:T(1,128)S(1)} fusion(f32[4096,2048]{0,1:T(8,128)} %subtract_subtract_fusion.1, f32[2048,1]{0,1:T(1,128)S(1)} %bitcast.331), kind=kOutput, calls=%fused_computation.255 | convolution fusion | flops 100663296 | bytes 33579008 | tf_op jit(solution)/shard_map/dot_general | solution.py:19
  744.7 33.1 %all-reduce.4 = (f32[4096]{0:T(1024)S(1)}, f32[4096]{0:T(1024)S(1)}) all-reduce(f32[4096]{0:T(1024)S(1)} %bitcast.287, f32[4096]{0:T(1024)S(1)} %bitcast.317), channel_id=1, replica_groups=mesh['row'=4,'col'=8] {'col'}, use_global_device_ids=true, to_apply=%region_36.37 | all-reduce | flops 8192 | bytes 65536 | tf_op jit(solution)/shard_map/psum | solution.py:54
  778.9 6.3 psum.189
  785.8 5.2 all_gather.61
  795.9 5.6 all_gather.62
  804.7 1.3 convolution_bitcast_fusion
  806.0 1.3 convolution_bitcast_fusion.1
  807.3 21.0 %fusion.135 = f32[1,4096]{1,0:T(1,128)S(1)} fusion(f32[4096,2048]{0,1:T(8,128)} %subtract_subtract_fusion.1, f32[2048,1]{0,1:T(1,128)S(1)} %bitcast.332), kind=kOutput, calls=%fused_computation.256 | convolution fusion | flops 100663296 | bytes 33579008 | tf_op jit(solution)/shard_map/dot_general | solution.py:19
  828.3 33.0 %psum.190 = f32[4096]{0:T(1024)S(1)} all-reduce(f32[4096]{0:T(1024)S(1)} %bitcast.288), channel_id=1, replica_groups=mesh['row'=4,'col'=8] {'col'}, use_global_device_ids=true, to_apply=%region_40.41 | all-reduce | flops 4096 | bytes 32768 | tf_op jit(solution)/shard_map/psum | solution.py:54
  863.7 6.3 psum.191
  870.6 5.5 all_gather.63
  877.2 30.1 %fusion.11 = f32[4096,2048]{0,1:T(8,128)} fusion(f32[16384,4]{0,1:T(4,128)S(1)} %scatter.76, s32[]{:T(128)S(6)} %select_n.183, f32[16384,4]{0,1:T(4,128)S(1)} %scatter.79, s32[]{:T(128)S(6)} %select_n.184), kind=kOutput, calls=%fused_computation.39 | convolution fusion | flops 402653184 | bytes 33652744 | tf_op jit(solution)/shard_map/dot_general | solution.py:19
  907.3 41.1 %subtract_subtract_fusion = f32[4096,2048]{0,1:T(8,128)} fusion(f32[4096,2048]{0,1:T(8,128)} %subtract_subtract_fusion.1, f32[4096,2048]{0,1:T(8,128)} %fusion.11, f32[16384,4]{0,1:T(4,128)S(1)} %scatter.79, s32[]{:T(128)S(6)} %select_n.183, f32[16384,4]{0,1:T(4,128)S(1)} %scatter.76, s32[]{:T(128)S(6)} %select_n.184), kind=kOutput, calls=%fused_computation | convolution fusion | flops 419430400 | bytes 100761608 | tf_op jit(solution)/shard_map/dot_general | solution.py:19
  948.4 33.3 %copy.49 = f32[4096,2048]{1,0:T(8,128)} copy(f32[4096,2048]{0,1:T(8,128)} %subtract_subtract_fusion) | data formatting | bytes 67108864 | tf_op jit(solution)/shard_map/sub | solution.py:72
  (123 shorter events, 51.4 us)
where the time goes:
time: 991 us; the launch traced here: 982 us
  blocking collectives  472 us (48%)
  matrix products  376 us (38%)
  local copies, waits for them, and re-layouts  87.7 us (9%)
  other arithmetic  24.6 us (2%)
  between operations  22 us (2%)
    dot_general x50, matrix products, product(): jnp.dot(left, right, precision=highest, preferred_element_type=jnp.float32)  376 us
    psum x8, blocking collectives, on_device(): summed = lax.psum(product(current, vector_cols), 'col')  264 us
    psum x2, blocking collectives, from_root(): return lax.psum(kept, axis)  71.8 us
    psum x8, blocking collectives, on_device(): inner = lax.psum(jnp.sum(mapped * vector_rows), 'row')  50.2 us
    all_gather x8, blocking collectives, on_device(): whole = lax.all_gather(column, 'row', axis=0, tiled=True)  43.5 us
    all_gather x8, blocking collectives, on_device(): lax.all_gather(mapped - 0.5 * factor * inner * vector_rows, 'row', axis=0...  42.4 us
    sub x1, local copies, waits for them, and re-layouts, on_device(): current - product(reflector_rows, update_cols.T)  33.3 us
    unnamed x1, local copies, waits for them, and re-layouts  31.1 us

commit v1 on v0

v1 whole, which is shorter than its diff:
```python
import functools
import math

import jax
import jax.numpy as jnp
from jax import lax
from jax.sharding import PartitionSpec as P
import jax.experimental.pallas as pl
import jax.experimental.pallas.tpu as pltpu

REFL = 4
PANELS = 2
STEPS = REFL * PANELS
LANES = 128
BLOCK = 256
SLOTS = 3
PIECES = 8
VMEM = pl.BlockSpec(memory_space=pltpu.VMEM)


def params(mib, **kw):
    return pltpu.CompilerParams(vmem_limit_bytes=mib << 20, **kw)


def total(x):
    return jnp.sum(jnp.sum(x, axis=0, keepdims=True), axis=1, keepdims=True)


def reflector(column, c):
    shape = column.shape
    row = lax.broadcasted_iota(jnp.int32, shape, 0)
    lane = lax.broadcasted_iota(jnp.int32, shape, 1)
    beneath = jnp.where((row > 0) | (lane > c), column, 0.0)
    length = jnp.sqrt(total(beneath * beneath))
    leading = column[0:1, c + 1 : c + 2]
    signed = jnp.where(leading >= 0.0, length, -length)
    vector = beneath + jnp.where((row == 0) & (lane == c + 1), signed, 0.0)
    return vector, 1.0 / (length * (length + jnp.abs(leading)))


def finish(y, vs, ws, factor):
    v = vs[-1]
    inner = total(y * v)
    rest = y
    for vj, wj in zip(vs[:-1], ws):
        on_w = total(wj * v)
        on_v = total(vj * v)
        rest = rest - vj * on_w - wj * on_v
        inner = inner - 2.0 * on_w * on_v
    return factor * rest - (0.5 * factor * factor * inner) * v


def whole_product(recv_ref, y_ref, row_size, col_size):
    half = recv_ref.shape[1]
    for c in range(col_size):
        for h in range(2):
            parts = [recv_ref[r * col_size + c] for r in range(h, row_size, 2)]
            s = parts[0]
            for p in parts[1:]:
                s = s + p
            y_ref[(c * 2 + h) * half : (c * 2 + h + 1) * half, :] = s


def partial_product(pieces, v_ref, c_ref, p_ref, keep_ref, send_ref, arrive=None):
    height, cols = pieces[0].shape
    tiles = cols // LANES
    lines = height * len(pieces) // LANES
    start = pl.multiple_of(lax.axis_index("row") * lines, 8)
    own = v_ref[pl.ds(start, lines), :]
    turned = jnp.concatenate([own] * (LANES // lines), axis=0).T
    for k in range(lines):
        c_ref[k * LANES : (k + 1) * LANES, :] = jnp.broadcast_to(turned[:, k : k + 1], (LANES, LANES))
    acc = (jnp.zeros((8, LANES), jnp.float32),) * tiles
    for index, a_ref in enumerate(pieces):
        if arrive is not None:
            arrive(index)

        def step(s, acc):
            base = pl.multiple_of(s * LANES, LANES)
            for k in range(0, LANES, 8):
                coef = c_ref[pl.ds(index * height + base + k, 8), :]
                acc = tuple(
                    acc[j] + a_ref[pl.ds(base + k, 8), j * LANES : (j + 1) * LANES] * coef
                    for j in range(tiles)
                )
            return acc

        acc = lax.fori_loop(0, height // LANES, step, acc)
    for j in range(tiles):
        p_ref[j : j + 1, :] = jnp.sum(acc[j], axis=0, keepdims=True)
    half = tiles // 2
    first = lax.axis_index("row") % 2 == 0
    low = p_ref[0:half, :]
    high = p_ref[half:tiles, :]
    keep_ref[...] = jnp.where(first, low, high)
    send_ref[...] = jnp.where(first, high, low)


def first_kernel(a_ref, recv_ref, *refs, count, col_size, shares):
    pieces = refs[:count]
    b_ref, v_ref, f_ref, keep_ref, send_ref, c_ref, p_ref, sems = refs[count:]
    height = pieces[0].shape[0]
    copies = [
        pltpu.make_async_copy(a_ref.at[k * height : (k + 1) * height], pieces[k], sems.at[k])
        for k in range(count)
    ]
    for copy in copies:
        copy.start()
    width = recv_ref.shape[2] // LANES
    for r in range(shares):
        for c in range(col_size):
            for q in range(width):
                b_ref[:, (c * shares + r) * width + q, :] = recv_ref[
                    r * col_size + c, :, q * LANES : (q + 1) * LANES
                ]
    v, factor = reflector(b_ref[0], 0)
    v_ref[...] = v
    f_ref[...] = jnp.broadcast_to(factor, f_ref.shape)
    partial_product(
        pieces, v_ref, c_ref, p_ref, keep_ref, send_ref, lambda k: copies[k].wait()
    )


def next_kernel(*refs, c, count, row_size, col_size):
    pieces = refs[:count]
    recv_ref, b_ref, of_ref = refs[count : count + 3]
    refs = refs[count + 3 :]
    vs = refs[:c]
    ws = refs[c : 2 * c - 1]
    w_ref, v_ref, f_ref, keep_ref, send_ref, y_ref, c_ref, p_ref = refs[2 * c - 1 :]
    whole_product(recv_ref, y_ref, row_size, col_size)
    vs = [r[...] for r in vs]
    ws = [r[...] for r in ws]
    w = finish(y_ref[...], vs, ws, of_ref[0:1, 0:1])
    w_ref[...] = w
    ws = ws + [w]
    column = b_ref[c]
    for vj, wj in zip(vs, ws):
        column = column - vj * wj[0:1, c : c + 1] - wj * vj[0:1, c : c + 1]
    v, factor = reflector(column, c)
    v_ref[...] = v
    f_ref[...] = jnp.broadcast_to(factor, f_ref.shape)
    partial_product(pieces, v_ref, c_ref, p_ref, keep_ref, send_ref)


def spread_kernel(keep_ref, got_ref, out_ref):
    out_ref[...] = jnp.broadcast_to((keep_ref[...] + got_ref[...])[None], out_ref.shape)


def thirds(x):
    hi = x.astype(jnp.bfloat16)
    rest = x - hi.astype(jnp.float32)
    mid = rest.astype(jnp.bfloat16)
    low = (rest - mid.astype(jnp.float32)).astype(jnp.bfloat16)
    return hi, mid, low


def last_kernel(*refs, count, row_size, col_size):
    pieces = refs[:count]
    recv_ref, of_ref = refs[count : count + 2]
    refs = refs[count + 2 :]
    vs = refs[:STEPS]
    ws = refs[STEPS : 2 * STEPS - 1]
    out_ref, y_ref, v_ref, w_ref, left_ref, right_ref, stage_ref, sems = refs[2 * STEPS - 1 :]
    height, cols = pieces[0].shape
    rows = height * count
    slots, block = stage_ref.shape[:2]
    whole_product(recv_ref, y_ref, row_size, col_size)
    v_all = [r[...] for r in vs]
    w_all = [r[...] for r in ws]
    w_all.append(finish(y_ref[...], v_all, w_all, of_ref[0:1, 0:1]))
    for j in range(STEPS):
        v_ref[j] = v_all[j]
        w_ref[j] = w_all[j]
    row_start = lax.axis_index("row") * (rows // LANES)
    for t in range(rows // LANES):
        v = v_ref[:, row_start + t, :]
        w = w_ref[:, row_start + t, :]
        hi, mid, low = thirds(jnp.concatenate([v, w], axis=0))
        left_ref[:, t * LANES : (t + 1) * LANES] = jnp.concatenate([hi, hi, mid, hi, mid, low], axis=0)
    col_start = lax.axis_index("col") * (cols // LANES)
    for t in range(cols // LANES):
        v = v_ref[:, col_start + t, :]
        w = w_ref[:, col_start + t, :]
        hi, mid, low = thirds(jnp.concatenate([w, v], axis=0))
        right_ref[:, t * LANES : (t + 1) * LANES] = jnp.concatenate([hi, mid, hi, low, mid, hi], axis=0)

    def copy(n):
        slot = n % slots
        return pltpu.make_async_copy(
            stage_ref.at[slot], out_ref.at[n * block : (n + 1) * block], sems.at[slot]
        )

    for n in range(rows // block):
        if n >= slots:
            copy(n - slots).wait()
        change = lax.dot_general(
            left_ref[:, n * block : (n + 1) * block],
            right_ref[...],
            (((0,), (0,)), ((), ())),
            preferred_element_type=jnp.float32,
        )
        at = n * block
        stage_ref[n % slots] = pieces[at // height][at % height : at % height + block, :] - change
        copy(n).start()
    for n in range(max(0, rows // block - slots), rows // block):
        copy(n).wait()


def f32(*shape):
    return jax.ShapeDtypeStruct(shape, jnp.float32)


def on_device(matrix):
    rows, cols = matrix.shape
    row_size = lax.axis_size("row")
    col_size = lax.axis_size("col")
    lines = rows * row_size // LANES
    tiles = cols // LANES
    both = ("row", "col")
    everyone = row_size * col_size
    pairs = [(i, i ^ 1) for i in range(row_size)]
    scratch = [pltpu.VMEM((rows, LANES), jnp.float32), pltpu.VMEM((tiles, LANES), jnp.float32)]
    state = [f32(lines, LANES), f32(8, LANES), f32(tiles // 2, LANES), f32(tiles // 2, LANES)]

    shares = math.gcd(row_size, tiles)
    width = cols // shares
    head = matrix[:STEPS, :].reshape(STEPS, shares, width).transpose(1, 0, 2)
    head = jnp.concatenate([head] * (row_size // shares), axis=0)
    mine = lax.all_to_all(head, "row", 0, 0, tiled=True)[0]
    heads = lax.all_to_all(
        jnp.broadcast_to(mine[None], (everyone,) + mine.shape), both, 0, 0, tiled=True
    )
    count = math.gcd(PIECES, rows // LANES)
    pieces = [pltpu.VMEM((rows // count, cols), jnp.float32)] * count

    def exchange(keep, send):
        got = lax.ppermute(send, "row", pairs)
        spread = pl.pallas_call(
            spread_kernel,
            out_shape=f32(everyone, *keep.shape),
            in_specs=[VMEM] * 2,
            out_specs=VMEM,
            compiler_params=params(4),
            name="spread",
        )(keep, got)
        return lax.all_to_all(spread, both, 0, 0, tiled=True)

    *held, top, v, factor, keep, send = pl.pallas_call(
        functools.partial(first_kernel, count=count, col_size=col_size, shares=shares),
        out_shape=pieces + [f32(STEPS, lines, LANES)] + state,
        in_specs=[pl.BlockSpec(memory_space=pl.ANY), VMEM],
        out_specs=[VMEM] * (count + 5),
        scratch_shapes=scratch + [pltpu.SemaphoreType.DMA((count,))],
        compiler_params=params(6),
        name="first",
    )(matrix, heads)
    vs, ws = [v], []
    for c in range(1, STEPS):
        recv = exchange(keep, send)
        w, v, factor, keep, send = pl.pallas_call(
            functools.partial(
                next_kernel, c=c, count=count, row_size=row_size, col_size=col_size
            ),
            out_shape=[f32(lines, LANES)] + state,
            in_specs=[VMEM] * (count + 2 + 2 * c),
            out_specs=[VMEM] * 5,
            scratch_shapes=[pltpu.VMEM((lines, LANES), jnp.float32)] + scratch,
            compiler_params=params(6),
            name=f"next{c}",
        )(*held, recv, top, factor, *vs, *ws)
        ws.append(w)
        vs.append(v)
    recv = exchange(keep, send)
    block = math.gcd(rows // count, BLOCK)
    return pl.pallas_call(
        functools.partial(last_kernel, count=count, row_size=row_size, col_size=col_size),
        out_shape=f32(rows, cols),
        in_specs=[VMEM] * (count + 1 + 2 * STEPS),
        out_specs=pl.BlockSpec(memory_space=pl.ANY),
        scratch_shapes=[
            pltpu.VMEM((lines, LANES), jnp.float32),
            pltpu.VMEM((STEPS, lines, LANES), jnp.float32),
            pltpu.VMEM((STEPS, lines, LANES), jnp.float32),
            pltpu.VMEM((12 * STEPS, rows), jnp.bfloat16),
            pltpu.VMEM((12 * STEPS, cols), jnp.bfloat16),
            pltpu.VMEM((SLOTS, block, cols), jnp.float32),
            pltpu.SemaphoreType.DMA((SLOTS,)),
        ],
        compiler_params=params(10),
        name="last",
    )(*held, recv, factor, *vs, *ws)


def solution(mesh):
    return jax.shard_map(
        on_device,
        mesh=mesh,
        in_specs=(P("row", "col"),),
        out_specs=P("row", "col"),
        check_vma=False,
    )
```

time: 991 us -> 169 us (0.17)
  matrix products: 376 us -> 0 us
  blocking collectives: 472 us -> 109 us
  local copies, waits for them, and re-layouts: 87.7 us -> 0.9 us
  Pallas kernels: 0 us -> 49.3 us
  other arithmetic: 24.6 us -> 0 us
  between operations: 22 us -> 0.24 us
    psum x18 -> x0, blocking collectives: 387 us -> none  [the longest x8 264 us: on_device(): summed = lax.psum(product(current, vector_cols), 'col')]
    dot_general x50 -> x0, matrix products: 376 us -> none  [product(): jnp.dot(left, right, precision=highest, preferred_element_type=jnp.float32)]
    all_to_all x0 -> x10, blocking collectives: none -> 109 us  [the longest x8 79.7 us: exchange(): return lax.all_to_all(spread, both, 0, 0, tiled=True)]
    all_gather x16 -> x0, blocking collectives: 85.8 us -> none  [the longest x8 43.5 us: on_device(): whole = lax.all_gather(column, 'row', axis=0, tiled=True)]
    pallas_call x0 -> x17, Pallas kernels: none -> 49.3 us  [the longest x7 26 us: on_device(): pl.pallas_call(functools.partial(next_kernel, c=c, count=count, row_size=...]
    sub x1 -> x0, local copies, waits for them, and re-layouts: 33.3 us -> none  [on_device(): current - product(reflector_rows, update_cols.T)]
    unnamed x1 -> x0, local copies, waits for them, and re-layouts: 31.1 us -> none
    scatter x16 -> x0, local copies, waits for them, and re-layouts: 14.2 us -> none  [the longest x8 7.16 us: on_device(): reflectors = reflectors.at[:, inner_index].set(vector)]
  transfers between devices with their start and end apart: 0 -> 8, of which waited for: 0 -> 8; matrix products, arithmetic and copies ran while one was open for 0% -> 0% of each run, Pallas kernels for 0% -> 0%
where the time goes in v1:
time: 169 us
  blocking collectives  109 us (64%)
  Pallas kernels  49.3 us (29%)
  waiting for transfers between devices  8.55 us (5%)
    all_to_all x8, blocking collectives, exchange(): return lax.all_to_all(spread, both, 0, 0, tiled=True)  79.7 us
    pallas_call x7, Pallas kernels, on_device(): pl.pallas_call(functools.partial(next_kernel, c=c, count=count, row_size=...  26 us
    all_to_all x1, blocking collectives, on_device(): lax.all_to_all(jnp.broadcast_to(mine[None], (everyone,) + mine.shape), bo...  20.9 us
    pallas_call x1, Pallas kernels, on_device(): pl.pallas_call(functools.partial(last_kernel, count=count, row_size=row_s...  11.9 us
    pallas_call x1, Pallas kernels, on_device(): pl.pallas_call(functools.partial(first_kernel, count=count, col_size=col_...  11.3 us
    ppermute x8, waiting for transfers between devices, exchange(): got = lax.ppermute(send, 'row', pairs)  8.55 us
    all_to_all x1, blocking collectives, on_device(): mine = lax.all_to_all(head, 'row', 0, 0, tiled=True)[0]  8.17 us
  transfers between devices with their start and end apart: 8, of which 8 were waited for; matrix products, arithmetic and copies ran while one was open for 0% of the time, Pallas kernels for 0%

profile of v1, /device:TPU:0, one launch (start us, length us, event | category | flops | bytes accessed | tf_op | source)
XLA Modules:
  0.0 169.1 jit_solution(5858261236872034388)
XLA Ops:
  0.0 0.8 slice.6
  0.8 8.2 %all_to_all.50 = f32[4,8,512]{2,1,0:T(8,128)S(1)} all-to-all(f32[4,8,512]{2,1,0:T(8,128)S(1)} %bitcast.5), channel_id=1, replica_groups=mesh['row'=4,'col'=8] {'row'}, dimensions={0} | all-to-all | bytes 131072 | tf_op jit(solution)/shard_map/all_to_all | solution.py:230
  9.0 0.1 broadcast_in_dim.8
  9.1 20.9 %all_to_all.51.recv_ref = f32[32,8,512]{2,1,0:T(8,128)S(1)} all-to-all(f32[32,8,512]{2,1,0:T(8,128)S(1)} %broadcast_in_dim.8), channel_id=1, replica_groups=mesh['row'=4,'col'=8] {'row','col'}, dimensions={0} | all-to-all | bytes 1048576 | tf_op jit(solution)/shard_map/all_to_all | solution.py:231
  30.0 11.3 %first.1 = (f32[512,2048]{1,0:T(8,128)S(1)}, f32[512,2048]{1,0:T(8,128)S(1)}, f32[512,2048]{1,0:T(8,128)S(1)}, f32[512,2048]{1,0:T(8,128)S(1)}, f32[512,2048]{1,...) custom-call(f32[4096,2048]{1,0:T(8,128)} %a_ref.1, ...), custom_call_target="tpu_custom_call" | custom-call | tf_op jit(solution)/shard_map/first/pallas_call | solution.py:249
  41.3 0.1 collective-permute-start
  41.4 1.2 collective-permute-done.got_ref
  42.5 10.0 %all_to_all.52.refs_8_ = f32[32,8,128]{2,1,0:T(8,128)S(1)} all-to-all(f32[32,8,128]{2,1,0:T(8,128)S(1)} %spread.8), channel_id=1, replica_groups=mesh['row'=4,'col'=8] {'row','col'}, dimensions={0} | all-to-all | bytes 262144 | tf_op jit(solution)/shard_map/all_to_all | solution.py:247
  52.5 3.7 %next1.1 = (f32[128,128]{1,0:T(8,128)S(1)}, f32[128,128]{1,0:T(8,128)S(1)}, f32[8,128]{1,0:T(8,128)S(1)}, f32[8,128]{1,0:T(8,128)S(1)}, f32[8,128]{1,0:T(8,128)S(1)}) custom-call(f32[512,2048]{1,0:T(8,128)S(1)} %get-tuple-element.53.refs_0_, f32[512,2048]{1,0:T(8,128)S(1)} %get-tuple-element.54.refs_1_, f32[512,2048]{1,0:T(8,128)S(1)} %get-tuple-element.55.refs_2_, ...), custom_call_target="tpu_custom_call" | custom-call | tf_op jit(solution)/shard_map/next1/pallas_call | solution.py:261
  56.2 0.2 collective-permute-start.1
  56.3 1.1 collective-permute-done.1.got_ref
  57.4 10.0 %all_to_all.53.refs_8_ = f32[32,8,128]{2,1,0:T(8,128)S(1)} all-to-all(f32[32,8,128]{2,1,0:T(8,128)S(1)} %spread.9), channel_id=1, replica_groups=mesh['row'=4,'col'=8] {'row','col'}, dimensions={0} | all-to-all | bytes 262144 | tf_op jit(solution)/shard_map/all_to_all | solution.py:247
  67.4 3.7 %next2.1 = (f32[128,128]{1,0:T(8,128)S(1)}, f32[128,128]{1,0:T(8,128)S(1)}, f32[8,128]{1,0:T(8,128)S(1)}, f32[8,128]{1,0:T(8,128)S(1)}, f32[8,128]{1,0:T(8,128)S(1)}) custom-call(f32[512,2048]{1,0:T(8,128)S(1)} %get-tuple-element.53.refs_0_, f32[512,2048]{1,0:T(8,128)S(1)} %get-tuple-element.54.refs_1_, f32[512,2048]{1,0:T(8,128)S(1)} %get-tuple-element.55.refs_2_, ...), custom_call_target="tpu_custom_call" | custom-call | tf_op jit(solution)/shard_map/next2/pallas_call | solution.py:261
  71.1 0.2 collective-permute-start.2
  71.2 1.1 collective-permute-done.2.got_ref
  72.3 10.0 %all_to_all.54.refs_8_ = f32[32,8,128]{2,1,0:T(8,128)S(1)} all-to-all(f32[32,8,128]{2,1,0:T(8,128)S(1)} %spread.10), channel_id=1, replica_groups=mesh['row'=4,'col'=8] {'row','col'}, dimensions={0} | all-to-all | bytes 262144 | tf_op jit(solution)/shard_map/all_to_all | solution.py:247
  82.3 3.7 %next3.1 = (f32[128,128]{1,0:T(8,128)S(1)}, f32[128,128]{1,0:T(8,128)S(1)}, f32[8,128]{1,0:T(8,128)S(1)}, f32[8,128]{1,0:T(8,128)S(1)}, f32[8,128]{1,0:T(8,128)S(1)}) custom-call(f32[512,2048]{1,0:T(8,128)S(1)} %get-tuple-element.53.refs_0_, f32[512,2048]{1,0:T(8,128)S(1)} %get-tuple-element.54.refs_1_, f32[512,2048]{1,0:T(8,128)S(1)} %get-tuple-element.55.refs_2_, ...), custom_call_target="tpu_custom_call" | custom-call | tf_op jit(solution)/shard_map/next3/pallas_call | solution.py:261
  86.0 0.2 collective-permute-start.3
  86.2 1.1 collective-permute-done.3.got_ref
  87.2 10.0 %all_to_all.55.refs_8_ = f32[32,8,128]{2,1,0:T(8,128)S(1)} all-to-all(f32[32,8,128]{2,1,0:T(8,128)S(1)} %spread.11), channel_id=1, replica_groups=mesh['row'=4,'col'=8] {'row','col'}, dimensions={0} | all-to-all | bytes 262144 | tf_op jit(solution)/shard_map/all_to_all | solution.py:247
  97.2 3.7 %next4.1 = (f32[128,128]{1,0:T(8,128)S(1)}, f32[128,128]{1,0:T(8,128)S(1)}, f32[8,128]{1,0:T(8,128)S(1)}, f32[8,128]{1,0:T(8,128)S(1)}, f32[8,128]{1,0:T(8,128)S(1)}) custom-call(f32[512,2048]{1,0:T(8,128)S(1)} %get-tuple-element.53.refs_0_, f32[512,2048]{1,0:T(8,128)S(1)} %get-tuple-element.54.refs_1_, f32[512,2048]{1,0:T(8,128)S(1)} %get-tuple-element.55.refs_2_, ...), custom_call_target="tpu_custom_call" | custom-call | tf_op jit(solution)/shard_map/next4/pallas_call | solution.py:261
  100.9 0.2 collective-permute-start.4
  101.1 1.1 collective-permute-done.4.got_ref
  102.1 10.0 %all_to_all.56.refs_8_ = f32[32,8,128]{2,1,0:T(8,128)S(1)} all-to-all(f32[32,8,128]{2,1,0:T(8,128)S(1)} %spread.12), channel_id=1, replica_groups=mesh['row'=4,'col'=8] {'row','col'}, dimensions={0} | all-to-all | bytes 262144 | tf_op jit(solution)/shard_map/all_to_all | solution.py:247
  112.1 3.7 %next5.1 = (f32[128,128]{1,0:T(8,128)S(1)}, f32[128,128]{1,0:T(8,128)S(1)}, f32[8,128]{1,0:T(8,128)S(1)}, f32[8,128]{1,0:T(8,128)S(1)}, f32[8,128]{1,0:T(8,128)S(1)}) custom-call(f32[512,2048]{1,0:T(8,128)S(1)} %get-tuple-element.53.refs_0_, f32[512,2048]{1,0:T(8,128)S(1)} %get-tuple-element.54.refs_1_, f32[512,2048]{1,0:T(8,128)S(1)} %get-tuple-element.55.refs_2_, ...), custom_call_target="tpu_custom_call" | custom-call | tf_op jit(solution)/shard_map/next5/pallas_call | solution.py:261
  115.9 0.2 collective-permute-start.5
  116.0 1.1 collective-permute-done.5.got_ref
  117.1 10.0 %all_to_all.57.refs_8_ = f32[32,8,128]{2,1,0:T(8,128)S(1)} all-to-all(f32[32,8,128]{2,1,0:T(8,128)S(1)} %spread.13), channel_id=1, replica_groups=mesh['row'=4,'col'=8] {'row','col'}, dimensions={0} | all-to-all | bytes 262144 | tf_op jit(solution)/shard_map/all_to_all | solution.py:247
  127.1 3.8 %next6.1 = (f32[128,128]{1,0:T(8,128)S(1)}, f32[128,128]{1,0:T(8,128)S(1)}, f32[8,128]{1,0:T(8,128)S(1)}, f32[8,128]{1,0:T(8,128)S(1)}, f32[8,128]{1,0:T(8,128)S(1)}) custom-call(f32[512,2048]{1,0:T(8,128)S(1)} %get-tuple-element.53.refs_0_, f32[512,2048]{1,0:T(8,128)S(1)} %get-tuple-element.54.refs_1_, f32[512,2048]{1,0:T(8,128)S(1)} %get-tuple-element.55.refs_2_, ...), custom_call_target="tpu_custom_call" | custom-call | tf_op jit(solution)/shard_map/next6/pallas_call | solution.py:261
  130.8 0.2 collective-permute-start.6
  131.0 1.1 collective-permute-done.6.got_ref
  132.1 10.0 %all_to_all.58.refs_8_ = f32[32,8,128]{2,1,0:T(8,128)S(1)} all-to-all(f32[32,8,128]{2,1,0:T(8,128)S(1)} %spread.14), channel_id=1, replica_groups=mesh['row'=4,'col'=8] {'row','col'}, dimensions={0} | all-to-all | bytes 262144 | tf_op jit(solution)/shard_map/all_to_all | solution.py:247
  142.1 3.8 %next7.1 = (f32[128,128]{1,0:T(8,128)S(1)}, f32[128,128]{1,0:T(8,128)S(1)}, f32[8,128]{1,0:T(8,128)S(1)}, f32[8,128]{1,0:T(8,128)S(1)}, f32[8,128]{1,0:T(8,128)S(1)}) custom-call(f32[512,2048]{1,0:T(8,128)S(1)} %get-tuple-element.53.refs_0_, f32[512,2048]{1,0:T(8,128)S(1)} %get-tuple-element.54.refs_1_, f32[512,2048]{1,0:T(8,128)S(1)} %get-tuple-element.55.refs_2_, ...), custom_call_target="tpu_custom_call" | custom-call | tf_op jit(solution)/shard_map/next7/pallas_call | solution.py:261
  145.8 0.2 collective-permute-start.7
  146.0 1.1 collective-permute-done.7.got_ref
  147.1 10.0 %all_to_all.59.refs_8_ = f32[32,8,128]{2,1,0:T(8,128)S(1)} all-to-all(f32[32,8,128]{2,1,0:T(8,128)S(1)} %spread.15), channel_id=1, replica_groups=mesh['row'=4,'col'=8] {'row','col'}, dimensions={0} | all-to-all | bytes 262144 | tf_op jit(solution)/shard_map/all_to_all | solution.py:247
  157.0 11.9 %last.1 = f32[4096,2048]{1,0:T(8,128)} custom-call(f32[512,2048]{1,0:T(8,128)S(1)} %get-tuple-element.53.refs_0_, f32[512,2048]{1,0:T(8,128)S(1)} %get-tuple-element.54.refs_1_, f32[512,2048]{1,0:T(8,128)S(1)} %get-tuple-element.55.refs_2_, f32[512,2048]{1,0:T(8,128)S(1)} %get-tuple-element.56.refs_3_, f32[512,2048]{1,0:T(8,128)S(1)} %get-tuple-element.57.refs_4_, ...), custom_call_target="tpu_custom_call" | custom-call | tf_op jit(solution)/shard_map/last/pallas_call | solution.py:276
  (9 shorter events, 0.1 us)
Async XLA Ops:
  41.3 1.2 collective-permute-start
  56.2 1.2 collective-permute-start.1
  71.1 1.2 collective-permute-start.2
  86.0 1.2 collective-permute-start.3
  100.9 1.2 collective-permute-start.4
  115.9 1.2 collective-permute-start.5
  130.8 1.2 collective-permute-start.6
  145.8 1.2 collective-permute-start.7

commit v2 on v1

--- a/solution.py
+++ b/solution.py
@@ -15,7 +15,10 @@
 BLOCK = 256
 SLOTS = 3
 PIECES = 8
+EARLY = 2
+MIDDLE = 4
 VMEM = pl.BlockSpec(memory_space=pltpu.VMEM)
+HBM = pl.BlockSpec(memory_space=pltpu.HBM)
 
 
 def params(mib, **kw):
@@ -96,28 +99,61 @@
     send_ref[...] = jnp.where(first, high, low)
 
 
-def first_kernel(a_ref, recv_ref, *refs, count, col_size, shares):
-    pieces = refs[:count]
-    b_ref, v_ref, f_ref, keep_ref, send_ref, c_ref, p_ref, sems = refs[count:]
+def piece_copies(a_ref, pieces, sems, start):
     height = pieces[0].shape[0]
-    copies = [
-        pltpu.make_async_copy(a_ref.at[k * height : (k + 1) * height], pieces[k], sems.at[k])
-        for k in range(count)
+    return [
+        pltpu.make_async_copy(
+            a_ref.at[(start + k) * height : (start + k + 1) * height], piece, sems.at[k]
+        )
+        for k, piece in enumerate(pieces)
     ]
+
+
+def load_kernel(a_ref, *refs, skip, start):
+    copies = piece_copies(a_ref, refs[skip:-1], refs[-1], start)
     for copy in copies:
         copy.start()
-    width = recv_ref.shape[2] // LANES
+    for copy in copies:
+        copy.wait()
+
+
+def head_kernel(*refs):
+    own_ref, out_ref = refs[1], refs[-1]
+    mine = jnp.where(lax.axis_index("row") == 0, own_ref[...], 0.0)
+    for got_ref in refs[2:-1]:
+        mine = mine + got_ref[...]
+    out_ref[...] = jnp.broadcast_to(mine[None], out_ref.shape)
+
+
+def first_kernel(a_ref, *refs, early, count, col_size, shares):
+    pieces = refs[:early]
+    near_ref, far_ref = refs[early : early + 2]
+    late = refs[early + 2 : count + 2]
+    b_ref, v_ref, f_ref, keep_ref, send_ref, c_ref, p_ref, sems = refs[count + 2 :]
+    copies = piece_copies(a_ref, late, sems, early)
+    for copy in copies:
+        copy.start()
+    pieces = pieces + late
+    width = near_ref.shape[2] // LANES
+    even = lax.axis_index("row") % 2 == 0
     for r in range(shares):
         for c in range(col_size):
+            near = near_ref[(r // 2) * col_size + c]
+            far = far_ref[(r // 2) * col_size + c]
+            piece = jnp.where(even, near, far) if r % 2 == 0 else jnp.where(even, far, near)
             for q in range(width):
-                b_ref[:, (c * shares + r) * width + q, :] = recv_ref[
-                    r * col_size + c, :, q * LANES : (q + 1) * LANES
-                ]
+                b_ref[:, (c * shares + r) * width + q, :] = piece[:, q * LANES : (q + 1) * LANES]
     v, factor = reflector(b_ref[0], 0)
     v_ref[...] = v
     f_ref[...] = jnp.broadcast_to(factor, f_ref.shape)
     partial_product(
-        pieces, v_ref, c_ref, p_ref, keep_ref, send_ref, lambda k: copies[k].wait()
+        pieces,
+        v_ref,
+        c_ref,
+        p_ref,
+        keep_ref,
+        send_ref,
+        lambda k: copies[k - early].wait() if k >= early else None,
     )
 
 
@@ -223,16 +259,51 @@
     scratch = [pltpu.VMEM((rows, LANES), jnp.float32), pltpu.VMEM((tiles, LANES), jnp.float32)]
     state = [f32(lines, LANES), f32(8, LANES), f32(tiles // 2, LANES), f32(tiles // 2, LANES)]
 
+    count = math.gcd(PIECES, rows // LANES)
+    pieces = [pltpu.VMEM((rows // count, cols), jnp.float32)] * count
+
     shares = math.gcd(row_size, tiles)
     width = cols // shares
-    head = matrix[:STEPS, :].reshape(STEPS, shares, width).transpose(1, 0, 2)
-    head = jnp.concatenate([head] * (row_size // shares), axis=0)
-    mine = lax.all_to_all(head, "row", 0, 0, tiled=True)[0]
-    heads = lax.all_to_all(
-        jnp.broadcast_to(mine[None], (everyone,) + mine.shape), both, 0, 0, tiled=True
-    )
-    count = math.gcd(PIECES, rows // LANES)
-    pieces = [pltpu.VMEM((rows // count, cols), jnp.float32)] * count
+    own = matrix[:STEPS, :width]
+    gots = []
+    for r in range(1, shares):
+        part = matrix[:STEPS, r * width : (r + 1) * width]
+        gots.append(lax.ppermute(part, "row", [(0, r)]))
+    early = min(EARLY, count - 1)
+    middle = min(MIDDLE, count - 1)
+
+    def load(start, stop, *after):
+        return pl.pallas_call(
+            functools.partial(load_kernel, skip=len(after), start=start),
+            out_shape=pieces[start:stop],
+            in_specs=[HBM] + [VMEM] * len(after),
+            out_specs=[VMEM] * (stop - start),
+            scratch_shapes=[pltpu.SemaphoreType.DMA((stop - start,))],
+            compiler_params=params(24),
+            cost_estimate=pl.CostEstimate(
+                flops=(stop - start) << 28, bytes_accessed=0, transcendentals=0
+            ),
+            name=f"load{start}",
+        )(matrix, *after)
+
+    loaded = load(0, early)
+    same = everyone // 2
+    heads = pl.pallas_call(
+        head_kernel,
+        out_shape=f32(same, STEPS, width),
+        in_specs=[VMEM] * (shares + 1),
+        out_specs=VMEM,
+        compiler_params=params(4),
+        name="head",
+    )(loaded[0], own, *gots)
+    groups = [
+        [r * col_size + c for r in range(core, row_size, 2) for c in range(col_size)]
+        for core in range(2)
+    ]
+    near = lax.all_to_all(heads, both, 0, 0, tiled=True, axis_index_groups=groups)
+    far = lax.ppermute(near, "row", pairs)
+    if middle > early:
+        loaded = [*loaded, *load(early, middle, near)]
 
     def exchange(keep, send):
         got = lax.ppermute(send, "row", pairs)
@@ -247,14 +318,17 @@
         return lax.all_to_all(spread, both, 0, 0, tiled=True)
 
     *held, top, v, factor, keep, send = pl.pallas_call(
-        functools.partial(first_kernel, count=count, col_size=col_size, shares=shares),
-        out_shape=pieces + [f32(STEPS, lines, LANES)] + state,
-        in_specs=[pl.BlockSpec(memory_space=pl.ANY), VMEM],
-        out_specs=[VMEM] * (count + 5),
-        scratch_shapes=scratch + [pltpu.SemaphoreType.DMA((count,))],
+        functools.partial(
+            first_kernel, early=middle, count=count, col_size=col_size, shares=shares
+        ),
+        out_shape=pieces[middle:] + [f32(STEPS, lines, LANES)] + state,
+        in_specs=[HBM] + [VMEM] * (middle + 2),
+        out_specs=[VMEM] * (count - middle + 5),
+        scratch_shapes=scratch + [pltpu.SemaphoreType.DMA((count - middle,))],
         compiler_params=params(6),
         name="first",
-    )(matrix, heads)
+    )(matrix, *loaded, near, far)
+    held = [*loaded, *held]
     vs, ws = [v], []
     for c in range(1, STEPS):
         recv = exchange(keep, send)
@@ -277,7 +351,7 @@
         functools.partial(last_kernel, count=count, row_size=row_size, col_size=col_size),
         out_shape=f32(rows, cols),
         in_specs=[VMEM] * (count + 1 + 2 * STEPS),
-        out_specs=pl.BlockSpec(memory_space=pl.ANY),
+        out_specs=HBM,
         scratch_shapes=[
             pltpu.VMEM((lines, LANES), jnp.float32),
             pltpu.VMEM((STEPS, lines, LANES), jnp.float32),

time: 169 us -> 164 us (0.970)
  blocking collectives: 109 us -> 93.9 us
  starting transfers between devices: 1.29 us -> 8.69 us
  Pallas kernels: 49.3 us -> 51.8 us
    all_to_all x2 -> x1, blocking collectives: 29.1 us -> 14.2 us  [on_device(): lax.all_to_all(heads, both, 0, 0, tiled=True, axis_index_groups=groups)]
    ppermute x0 -> x4, starting transfers between devices: none -> 6.91 us  [the longest x3 6.91 us: on_device(): gots.append(lax.ppermute(part, 'row', [(0, r)]))]
    pallas_call x1 -> x4, Pallas kernels: 11.3 us -> 13.4 us  [the longest x2 6.97 us: load(): pl.pallas_call(functools.partial(load_kernel, skip=len(after), start=star...]
  transfers between devices with their start and end apart: 8 -> 12, of which waited for: 8 -> 8; matrix products, arithmetic and copies ran while one was open for 0% -> 0% of each run, Pallas kernels for 0% -> 4%
where the time goes in v2:
time: 164 us
  blocking collectives  93.9 us (57%)
  Pallas kernels  51.8 us (32%)
  starting transfers between devices  8.69 us (5%)
  waiting for transfers between devices  8.24 us (5%)
    all_to_all x8, blocking collectives, exchange(): return lax.all_to_all(spread, both, 0, 0, tiled=True)  79.7 us
    pallas_call x7, Pallas kernels, on_device(): pl.pallas_call(functools.partial(next_kernel, c=c, count=count, row_size=...  26.5 us
    all_to_all x1, blocking collectives, on_device(): lax.all_to_all(heads, both, 0, 0, tiled=True, axis_index_groups=groups)  14.2 us
    pallas_call x1, Pallas kernels, on_device(): pl.pallas_call(functools.partial(last_kernel, count=count, row_size=row_s...  11.9 us
    ppermute x8, waiting for transfers between devices, exchange(): got = lax.ppermute(send, 'row', pairs)  8.22 us
    pallas_call x2, Pallas kernels, load(): pl.pallas_call(functools.partial(load_kernel, skip=len(after), start=star...  6.97 us
    ppermute x3, starting transfers between devices, on_device(): gots.append(lax.ppermute(part, 'row', [(0, r)]))  6.91 us
    pallas_call x1, Pallas kernels, on_device(): pl.pallas_call(functools.partial(first_kernel, early=middle, count=count,...  6.36 us
  transfers between devices with their start and end apart: 12, of which 8 were waited for; matrix products, arithmetic and copies ran while one was open for 0% of the time, Pallas kernels for 4%

profile of v2, /device:TPU:0, one launch (start us, length us, event | category | flops | bytes accessed | tf_op | source)
XLA Modules:
  0.0 163.7 jit_solution(2970225132675965490)
XLA Ops:
  0.0 0.8 fusion
  0.8 4.3 %collective-permute-start.2 = (f32[8,512]{1,0:T(8,128)S(1)}, f32[8,512]{1,0:T(8,128)S(1)}, u32[]{:S(2)}, u32[]{:S(2)}) collective-permute-start(f32[8,512]{1,0:T(8,128)S(1)} %get-tuple-element.101), channel_id=1, source_target_pairs={{0,24},{1,25},{2,26},{3,27},{4,28},{5,29},{6,30},{7,31}} | collective-permute-start | bytes 49160 | tf_op jit(solution)/shard_map/ppermute | solution.py:271
  5.1 1.3 collective-permute-start.1
  6.4 1.3 collective-permute-start
  7.7 3.5 %load0.1 = (f32[512,2048]{1,0:T(8,128)S(1)}, f32[512,2048]{1,0:T(8,128)S(1)}) custom-call(f32[4096,2048]{1,0:T(8,128)} %a_ref.5), custom_call_target="tpu_custom_call" | custom-call | flops 536870912 | tf_op jit(solution)/shard_map/load0/pallas_call | solution.py:276
  11.2 0.0 collective-permute-done.2.refs_4_
  11.2 0.0 collective-permute-done.1.refs_3_
  11.2 0.0 collective-permute-done.refs_2_
  11.3 14.2 %all_to_all.45.refs_0_.refs_4_ = f32[16,8,512]{2,1,0:T(8,128)S(1)} all-to-all(f32[16,8,512]{2,1,0:T(8,128)S(1)} %head.1), channel_id=1, replica_groups={{0,1,2,3,4,5,6,7,16,17,18,19,20,21,22,23},{8,9,10,11,12,13,14,15,24,25,..., dimensions={0} | all-to-all | bytes 524288 | tf_op jit(solution)/shard_map/all_to_all | solution.py:303
  25.5 0.0 collective-permute-start.3
  25.5 3.5 %load2.1 = (f32[512,2048]{1,0:T(8,128)S(1)}, f32[512,2048]{1,0:T(8,128)S(1)}) custom-call(f32[4096,2048]{1,0:T(8,128)} %a_ref.5, f32[16,8,512]{2,1,0:T(8,128)S(1)} %all_to_all.45.refs_0_.refs_4_), custom_call_target="tpu_custom_call" | custom-call | flops 536870912 | tf_op jit(solution)/shard_map/load2/pallas_call | solution.py:276
  29.0 0.0 collective-permute-done.3.refs_5_
  29.0 6.4 %first.1 = (f32[512,2048]{1,0:T(8,128)S(1)}, f32[512,2048]{1,0:T(8,128)S(1)}, f32[512,2048]{1,0:T(8,128)S(1)}, f32[512,2048]{1,0:T(8,128)S(1)}, f32[8,128,128]{2...) custom-call(f32[4096,2048]{1,0:T(8,128)} %a_ref.5, ...), custom_call_target="tpu_custom_call" | custom-call | tf_op jit(solution)/shard_map/first/pallas_call | solution.py:320
  35.4 0.6 collective-permute-start.4
  35.9 0.8 collective-permute-done.4.got_ref
  36.8 9.9 %all_to_all.46.refs_8_ = f32[32,8,128]{2,1,0:T(8,128)S(1)} all-to-all(f32[32,8,128]{2,1,0:T(8,128)S(1)} %spread.8), channel_id=1, replica_groups=mesh['row'=4,'col'=8] {'row','col'}, dimensions={0} | all-to-all | bytes 262144 | tf_op jit(solution)/shard_map/all_to_all | solution.py:318
  46.7 3.8 %next1.1 = (f32[128,128]{1,0:T(8,128)S(1)}, f32[128,128]{1,0:T(8,128)S(1)}, f32[8,128]{1,0:T(8,128)S(1)}, f32[8,128]{1,0:T(8,128)S(1)}, f32[8,128]{1,0:T(8,128)S(1)}) custom-call(f32[512,2048]{1,0:T(8,128)S(1)} %get-tuple-element.53.refs_0_, f32[512,2048]{1,0:T(8,128)S(1)} %get-tuple-element.54.refs_1_, f32[512,2048]{1,0:T(8,128)S(1)} %get-tuple-element.55.refs_2_, ...), custom_call_target="tpu_custom_call" | custom-call | tf_op jit(solution)/shard_map/next1/pallas_call | solution.py:335
  50.5 0.2 collective-permute-start.5
  50.6 1.1 collective-permute-done.5.got_ref
  51.7 10.0 %all_to_all.47.refs_8_ = f32[32,8,128]{2,1,0:T(8,128)S(1)} all-to-all(f32[32,8,128]{2,1,0:T(8,128)S(1)} %spread.9), channel_id=1, replica_groups=mesh['row'=4,'col'=8] {'row','col'}, dimensions={0} | all-to-all | bytes 262144 | tf_op jit(solution)/shard_map/all_to_all | solution.py:318
  61.7 3.8 %next2.1 = (f32[128,128]{1,0:T(8,128)S(1)}, f32[128,128]{1,0:T(8,128)S(1)}, f32[8,128]{1,0:T(8,128)S(1)}, f32[8,128]{1,0:T(8,128)S(1)}, f32[8,128]{1,0:T(8,128)S(1)}) custom-call(f32[512,2048]{1,0:T(8,128)S(1)} %get-tuple-element.53.refs_0_, f32[512,2048]{1,0:T(8,128)S(1)} %get-tuple-element.54.refs_1_, f32[512,2048]{1,0:T(8,128)S(1)} %get-tuple-element.55.refs_2_, ...), custom_call_target="tpu_custom_call" | custom-call | tf_op jit(solution)/shard_map/next2/pallas_call | solution.py:335
  65.4 0.2 collective-permute-start.6
  65.6 1.1 collective-permute-done.6.got_ref
  66.7 10.0 %all_to_all.48.refs_8_ = f32[32,8,128]{2,1,0:T(8,128)S(1)} all-to-all(f32[32,8,128]{2,1,0:T(8,128)S(1)} %spread.10), channel_id=1, replica_groups=mesh['row'=4,'col'=8] {'row','col'}, dimensions={0} | all-to-all | bytes 262144 | tf_op jit(solution)/shard_map/all_to_all | solution.py:318
  76.7 3.8 %next3.1 = (f32[128,128]{1,0:T(8,128)S(1)}, f32[128,128]{1,0:T(8,128)S(1)}, f32[8,128]{1,0:T(8,128)S(1)}, f32[8,128]{1,0:T(8,128)S(1)}, f32[8,128]{1,0:T(8,128)S(1)}) custom-call(f32[512,2048]{1,0:T(8,128)S(1)} %get-tuple-element.53.refs_0_, f32[512,2048]{1,0:T(8,128)S(1)} %get-tuple-element.54.refs_1_, f32[512,2048]{1,0:T(8,128)S(1)} %get-tuple-element.55.refs_2_, ...), custom_call_target="tpu_custom_call" | custom-call | tf_op jit(solution)/shard_map/next3/pallas_call | solution.py:335
  80.4 0.2 collective-permute-start.7
  80.6 1.1 collective-permute-done.7.got_ref
  81.7 10.0 %all_to_all.49.refs_8_ = f32[32,8,128]{2,1,0:T(8,128)S(1)} all-to-all(f32[32,8,128]{2,1,0:T(8,128)S(1)} %spread.11), channel_id=1, replica_groups=mesh['row'=4,'col'=8] {'row','col'}, dimensions={0} | all-to-all | bytes 262144 | tf_op jit(solution)/shard_map/all_to_all | solution.py:318
  91.6 3.8 %next4.1 = (f32[128,128]{1,0:T(8,128)S(1)}, f32[128,128]{1,0:T(8,128)S(1)}, f32[8,128]{1,0:T(8,128)S(1)}, f32[8,128]{1,0:T(8,128)S(1)}, f32[8,128]{1,0:T(8,128)S(1)}) custom-call(f32[512,2048]{1,0:T(8,128)S(1)} %get-tuple-element.53.refs_0_, f32[512,2048]{1,0:T(8,128)S(1)} %get-tuple-element.54.refs_1_, f32[512,2048]{1,0:T(8,128)S(1)} %get-tuple-element.55.refs_2_, ...), custom_call_target="tpu_custom_call" | custom-call | tf_op jit(solution)/shard_map/next4/pallas_call | solution.py:335
  95.4 0.2 collective-permute-start.8
  95.6 1.1 collective-permute-done.8.got_ref
  96.7 10.0 %all_to_all.50.refs_8_ = f32[32,8,128]{2,1,0:T(8,128)S(1)} all-to-all(f32[32,8,128]{2,1,0:T(8,128)S(1)} %spread.12), channel_id=1, replica_groups=mesh['row'=4,'col'=8] {'row','col'}, dimensions={0} | all-to-all | bytes 262144 | tf_op jit(solution)/shard_map/all_to_all | solution.py:318
  106.6 3.8 %next5.1 = (f32[128,128]{1,0:T(8,128)S(1)}, f32[128,128]{1,0:T(8,128)S(1)}, f32[8,128]{1,0:T(8,128)S(1)}, f32[8,128]{1,0:T(8,128)S(1)}, f32[8,128]{1,0:T(8,128)S(1)}) custom-call(f32[512,2048]{1,0:T(8,128)S(1)} %get-tuple-element.53.refs_0_, f32[512,2048]{1,0:T(8,128)S(1)} %get-tuple-element.54.refs_1_, f32[512,2048]{1,0:T(8,128)S(1)} %get-tuple-element.55.refs_2_, ...), custom_call_target="tpu_custom_call" | custom-call | tf_op jit(solution)/shard_map/next5/pallas_call | solution.py:335
  110.4 0.2 collective-permute-start.9
  110.6 1.1 collective-permute-done.9.got_ref
  111.7 10.0 %all_to_all.51.refs_8_ = f32[32,8,128]{2,1,0:T(8,128)S(1)} all-to-all(f32[32,8,128]{2,1,0:T(8,128)S(1)} %spread.13), channel_id=1, replica_groups=mesh['row'=4,'col'=8] {'row','col'}, dimensions={0} | all-to-all | bytes 262144 | tf_op jit(solution)/shard_map/all_to_all | solution.py:318
  121.7 3.8 %next6.1 = (f32[128,128]{1,0:T(8,128)S(1)}, f32[128,128]{1,0:T(8,128)S(1)}, f32[8,128]{1,0:T(8,128)S(1)}, f32[8,128]{1,0:T(8,128)S(1)}, f32[8,128]{1,0:T(8,128)S(1)}) custom-call(f32[512,2048]{1,0:T(8,128)S(1)} %get-tuple-element.53.refs_0_, f32[512,2048]{1,0:T(8,128)S(1)} %get-tuple-element.54.refs_1_, f32[512,2048]{1,0:T(8,128)S(1)} %get-tuple-element.55.refs_2_, ...), custom_call_target="tpu_custom_call" | custom-call | tf_op jit(solution)/shard_map/next6/pallas_call | solution.py:335
  125.4 0.2 collective-permute-start.10
  125.6 1.1 collective-permute-done.10.got_ref
  126.7 10.0 %all_to_all.52.refs_8_ = f32[32,8,128]{2,1,0:T(8,128)S(1)} all-to-all(f32[32,8,128]{2,1,0:T(8,128)S(1)} %spread.14), channel_id=1, replica_groups=mesh['row'=4,'col'=8] {'row','col'}, dimensions={0} | all-to-all | bytes 262144 | tf_op jit(solution)/shard_map/all_to_all | solution.py:318
  136.7 3.8 %next7.1 = (f32[128,128]{1,0:T(8,128)S(1)}, f32[128,128]{1,0:T(8,128)S(1)}, f32[8,128]{1,0:T(8,128)S(1)}, f32[8,128]{1,0:T(8,128)S(1)}, f32[8,128]{1,0:T(8,128)S(1)}) custom-call(f32[512,2048]{1,0:T(8,128)S(1)} %get-tuple-element.53.refs_0_, f32[512,2048]{1,0:T(8,128)S(1)} %get-tuple-element.54.refs_1_, f32[512,2048]{1,0:T(8,128)S(1)} %get-tuple-element.55.refs_2_, ...), custom_call_target="tpu_custom_call" | custom-call | tf_op jit(solution)/shard_map/next7/pallas_call | solution.py:335
  140.5 0.2 collective-permute-start.11
  140.6 1.1 collective-permute-done.11.got_ref
  141.7 10.0 %all_to_all.53.refs_8_ = f32[32,8,128]{2,1,0:T(8,128)S(1)} all-to-all(f32[32,8,128]{2,1,0:T(8,128)S(1)} %spread.15), channel_id=1, replica_groups=mesh['row'=4,'col'=8] {'row','col'}, dimensions={0} | all-to-all | bytes 262144 | tf_op jit(solution)/shard_map/all_to_all | solution.py:318
  151.7 11.9 %last.1 = f32[4096,2048]{1,0:T(8,128)} custom-call(f32[512,2048]{1,0:T(8,128)S(1)} %get-tuple-element.53.refs_0_, f32[512,2048]{1,0:T(8,128)S(1)} %get-tuple-element.54.refs_1_, f32[512,2048]{1,0:T(8,128)S(1)} %get-tuple-element.55.refs_2_, f32[512,2048]{1,0:T(8,128)S(1)} %get-tuple-element.56.refs_3_, f32[512,2048]{1,0:T(8,128)S(1)} %get-tuple-element.57.refs_4_, ...), custom_call_target="tpu_custom_call" | custom-call | tf_op jit(solution)/shard_map/last/pallas_call | solution.py:350
  (9 shorter events, 0.1 us)
Async XLA Ops:
  0.8 10.4 %collective-permute-start.2 = (f32[8,512]{1,0:T(8,128)S(1)}, f32[8,512]{1,0:T(8,128)S(1)}, u32[]{:S(2)}, u32[]{:S(2)}) collective-permute-start(f32[8,512]{1,0:T(8,128)S(1)} %get-tuple-element.101), channel_id=1, source_target_pairs={{0,24},{1,25},{2,26},{3,27},{4,28},{5,29},{6,30},{7,31}} | collective-permute-start | bytes 49160 | tf_op jit(solution)/shard_map/ppermute | solution.py:271
  5.1 6.1 %collective-permute-start.1 = (f32[8,512]{1,0:T(8,128)S(1)}, f32[8,512]{1,0:T(8,128)S(1)}, u32[]{:S(2)}, u32[]{:S(2)}) collective-permute-start(f32[8,512]{1,0:T(8,128)S(1)} %get-tuple-element.102), channel_id=1, source_target_pairs={{0,16},{1,17},{2,18},{3,19},{4,20},{5,21},{6,22},{7,23}} | collective-permute-start | bytes 49160 | tf_op jit(solution)/shard_map/ppermute | solution.py:271
  6.4 4.8 %collective-permute-start = (f32[8,512]{1,0:T(8,128)S(1)}, f32[8,512]{1,0:T(8,128)S(1)}, u32[]{:S(2)}, u32[]{:S(2)}) collective-permute-start(f32[8,512]{1,0:T(8,128)S(1)} %get-tuple-element.103), channel_id=1, source_target_pairs={{0,8},{1,9},{2,10},{3,11},{4,12},{5,13},{6,14},{7,15}} | collective-permute-start | bytes 49160 | tf_op jit(solution)/shard_map/ppermute | solution.py:271
  25.5 3.5 %collective-permute-start.3 = (f32[16,8,512]{2,1,0:T(8,128)S(1)}, f32[16,8,512]{2,1,0:T(8,128)S(1)}, u32[]{:S(2)}, u32[]{:S(2)}) collective-permute-start(f32[16,8,512]{2,1,0:T(8,128)S(1)} %all_to_all.45.refs_0_.refs_4_), channel_id=1, source_target_pairs={{0,8},{8,0},{16,24},{24,16},{1,9},{9,1},{17,25},{25,17},{2,10},{10... | collective-permute-start | bytes 786440 | tf_op jit(solution)/shard_map/ppermute | solution.py:304
  35.4 1.4 collective-permute-start.4
  50.5 1.2 collective-permute-start.5
  65.4 1.2 collective-permute-start.6
  80.4 1.2 collective-permute-start.7
  95.4 1.2 collective-permute-start.8
  110.4 1.2 collective-permute-start.9
  125.4 1.2 collective-permute-start.10
  140.5 1.2 collective-permute-start.11

commit v3 on v2

--- a/solution.py
+++ b/solution.py
@@ -55,13 +55,19 @@
 
 def whole_product(recv_ref, y_ref, row_size, col_size):
     half = recv_ref.shape[1]
+    sums = []
     for c in range(col_size):
         for h in range(2):
             parts = [recv_ref[r * col_size + c] for r in range(h, row_size, 2)]
             s = parts[0]
             for p in parts[1:]:
                 s = s + p
-            y_ref[(c * 2 + h) * half : (c * 2 + h + 1) * half, :] = s
+            sums.append(s)
+    if half % 8 == 0:
+        return jnp.concatenate(sums, axis=0)
+    for k, s in enumerate(sums):
+        y_ref[k * half : (k + 1) * half, :] = s
+    return y_ref[...]
 
 
 def partial_product(pieces, v_ref, c_ref, p_ref, keep_ref, send_ref, arrive=None):
@@ -164,10 +170,10 @@
     vs = refs[:c]
     ws = refs[c : 2 * c - 1]
     w_ref, v_ref, f_ref, keep_ref, send_ref, y_ref, c_ref, p_ref = refs[2 * c - 1 :]
-    whole_product(recv_ref, y_ref, row_size, col_size)
+    y = whole_product(recv_ref, y_ref, row_size, col_size)
     vs = [r[...] for r in vs]
     ws = [r[...] for r in ws]
-    w = finish(y_ref[...], vs, ws, of_ref[0:1, 0:1])
+    w = finish(y, vs, ws, of_ref[0:1, 0:1])
     w_ref[...] = w
     ws = ws + [w]
     column = b_ref[c]
@@ -201,10 +207,10 @@
     height, cols = pieces[0].shape
     rows = height * count
     slots, block = stage_ref.shape[:2]
-    whole_product(recv_ref, y_ref, row_size, col_size)
+    y = whole_product(recv_ref, y_ref, row_size, col_size)
     v_all = [r[...] for r in vs]
     w_all = [r[...] for r in ws]
-    w_all.append(finish(y_ref[...], v_all, w_all, of_ref[0:1, 0:1]))
+    w_all.append(finish(y, v_all, w_all, of_ref[0:1, 0:1]))
     for j in range(STEPS):
         v_ref[j] = v_all[j]
         w_ref[j] = w_all[j]

time: 164 us -> 164 us (level)
  no operation moved by 1% of the time
where the time goes in v3:
time: 164 us
  blocking collectives  93.9 us (57%)
  Pallas kernels  51.8 us (32%)
  starting transfers between devices  8.69 us (5%)
  waiting for transfers between devices  8.24 us (5%)
    all_to_all x8, blocking collectives, exchange(): return lax.all_to_all(spread, both, 0, 0, tiled=True)  79.7 us
    pallas_call x7, Pallas kernels, on_device(): pl.pallas_call(functools.partial(next_kernel, c=c, count=count, row_size=...  26.5 us
    all_to_all x1, blocking collectives, on_device(): lax.all_to_all(heads, both, 0, 0, tiled=True, axis_index_groups=groups)  14.2 us
    pallas_call x1, Pallas kernels, on_device(): pl.pallas_call(functools.partial(last_kernel, count=count, row_size=row_s...  11.9 us
    ppermute x8, waiting for transfers between devices, exchange(): got = lax.ppermute(send, 'row', pairs)  8.22 us
    pallas_call x2, Pallas kernels, load(): pl.pallas_call(functools.partial(load_kernel, skip=len(after), start=star...  6.97 us
    ppermute x3, starting transfers between devices, on_device(): gots.append(lax.ppermute(part, 'row', [(0, r)]))  6.91 us
    pallas_call x1, Pallas kernels, on_device(): pl.pallas_call(functools.partial(first_kernel, early=middle, count=count,...  6.36 us
  transfers between devices with their start and end apart: 12, of which 8 were waited for; matrix products, arithmetic and copies ran while one was open for 0% of the time, Pallas kernels for 4%

profile of v3, /device:TPU:0, one launch (start us, length us, event | category | flops | bytes accessed | tf_op | source)
XLA Modules:
  0.0 163.7 jit_solution(2970225132675965490)
XLA Ops:
  0.0 0.8 fusion
  0.8 4.3 %collective-permute-start.2 = (f32[8,512]{1,0:T(8,128)S(1)}, f32[8,512]{1,0:T(8,128)S(1)}, u32[]{:S(2)}, u32[]{:S(2)}) collective-permute-start(f32[8,512]{1,0:T(8,128)S(1)} %get-tuple-element.101), channel_id=1, source_target_pairs={{0,24},{1,25},{2,26},{3,27},{4,28},{5,29},{6,30},{7,31}} | collective-permute-start | bytes 49160 | tf_op jit(solution)/shard_map/ppermute | solution.py:277
  5.1 1.3 collective-permute-start.1
  6.4 1.3 collective-permute-start
  7.7 3.5 %load0.1 = (f32[512,2048]{1,0:T(8,128)S(1)}, f32[512,2048]{1,0:T(8,128)S(1)}) custom-call(f32[4096,2048]{1,0:T(8,128)} %a_ref.5), custom_call_target="tpu_custom_call" | custom-call | flops 536870912 | tf_op jit(solution)/shard_map/load0/pallas_call | solution.py:282
  11.2 0.0 collective-permute-done.2.refs_4_
  11.2 0.0 collective-permute-done.1.refs_3_
  11.2 0.0 collective-permute-done.refs_2_
  11.3 14.2 %all_to_all.45.refs_0_.refs_4_ = f32[16,8,512]{2,1,0:T(8,128)S(1)} all-to-all(f32[16,8,512]{2,1,0:T(8,128)S(1)} %head.1), channel_id=1, replica_groups={{0,1,2,3,4,5,6,7,16,17,18,19,20,21,22,23},{8,9,10,11,12,13,14,15,24,25,..., dimensions={0} | all-to-all | bytes 524288 | tf_op jit(solution)/shard_map/all_to_all | solution.py:309
  25.5 0.0 collective-permute-start.3
  25.5 3.5 %load2.1 = (f32[512,2048]{1,0:T(8,128)S(1)}, f32[512,2048]{1,0:T(8,128)S(1)}) custom-call(f32[4096,2048]{1,0:T(8,128)} %a_ref.5, f32[16,8,512]{2,1,0:T(8,128)S(1)} %all_to_all.45.refs_0_.refs_4_), custom_call_target="tpu_custom_call" | custom-call | flops 536870912 | tf_op jit(solution)/shard_map/load2/pallas_call | solution.py:282
  29.0 0.0 collective-permute-done.3.refs_5_
  29.0 6.4 %first.1 = (f32[512,2048]{1,0:T(8,128)S(1)}, f32[512,2048]{1,0:T(8,128)S(1)}, f32[512,2048]{1,0:T(8,128)S(1)}, f32[512,2048]{1,0:T(8,128)S(1)}, f32[8,128,128]{2...) custom-call(f32[4096,2048]{1,0:T(8,128)} %a_ref.5, ...), custom_call_target="tpu_custom_call" | custom-call | tf_op jit(solution)/shard_map/first/pallas_call | solution.py:326
  35.4 0.6 collective-permute-start.4
  35.9 0.8 collective-permute-done.4.got_ref
  36.8 9.9 %all_to_all.46.refs_8_ = f32[32,8,128]{2,1,0:T(8,128)S(1)} all-to-all(f32[32,8,128]{2,1,0:T(8,128)S(1)} %spread.8), channel_id=1, replica_groups=mesh['row'=4,'col'=8] {'row','col'}, dimensions={0} | all-to-all | bytes 262144 | tf_op jit(solution)/shard_map/all_to_all | solution.py:324
  46.7 3.8 %next1.1 = (f32[128,128]{1,0:T(8,128)S(1)}, f32[128,128]{1,0:T(8,128)S(1)}, f32[8,128]{1,0:T(8,128)S(1)}, f32[8,128]{1,0:T(8,128)S(1)}, f32[8,128]{1,0:T(8,128)S(1)}) custom-call(f32[512,2048]{1,0:T(8,128)S(1)} %get-tuple-element.53.refs_0_, f32[512,2048]{1,0:T(8,128)S(1)} %get-tuple-element.54.refs_1_, f32[512,2048]{1,0:T(8,128)S(1)} %get-tuple-element.55.refs_2_, ...), custom_call_target="tpu_custom_call" | custom-call | tf_op jit(solution)/shard_map/next1/pallas_call | solution.py:341
  50.5 0.2 collective-permute-start.5
  50.6 1.1 collective-permute-done.5.got_ref
  51.7 10.0 %all_to_all.47.refs_8_ = f32[32,8,128]{2,1,0:T(8,128)S(1)} all-to-all(f32[32,8,128]{2,1,0:T(8,128)S(1)} %spread.9), channel_id=1, replica_groups=mesh['row'=4,'col'=8] {'row','col'}, dimensions={0} | all-to-all | bytes 262144 | tf_op jit(solution)/shard_map/all_to_all | solution.py:324
  61.7 3.8 %next2.1 = (f32[128,128]{1,0:T(8,128)S(1)}, f32[128,128]{1,0:T(8,128)S(1)}, f32[8,128]{1,0:T(8,128)S(1)}, f32[8,128]{1,0:T(8,128)S(1)}, f32[8,128]{1,0:T(8,128)S(1)}) custom-call(f32[512,2048]{1,0:T(8,128)S(1)} %get-tuple-element.53.refs_0_, f32[512,2048]{1,0:T(8,128)S(1)} %get-tuple-element.54.refs_1_, f32[512,2048]{1,0:T(8,128)S(1)} %get-tuple-element.55.refs_2_, ...), custom_call_target="tpu_custom_call" | custom-call | tf_op jit(solution)/shard_map/next2/pallas_call | solution.py:341
  65.4 0.2 collective-permute-start.6
  65.6 1.1 collective-permute-done.6.got_ref
  66.7 10.0 %all_to_all.48.refs_8_ = f32[32,8,128]{2,1,0:T(8,128)S(1)} all-to-all(f32[32,8,128]{2,1,0:T(8,128)S(1)} %spread.10), channel_id=1, replica_groups=mesh['row'=4,'col'=8] {'row','col'}, dimensions={0} | all-to-all | bytes 262144 | tf_op jit(solution)/shard_map/all_to_all | solution.py:324
  76.7 3.8 %next3.1 = (f32[128,128]{1,0:T(8,128)S(1)}, f32[128,128]{1,0:T(8,128)S(1)}, f32[8,128]{1,0:T(8,128)S(1)}, f32[8,128]{1,0:T(8,128)S(1)}, f32[8,128]{1,0:T(8,128)S(1)}) custom-call(f32[512,2048]{1,0:T(8,128)S(1)} %get-tuple-element.53.refs_0_, f32[512,2048]{1,0:T(8,128)S(1)} %get-tuple-element.54.refs_1_, f32[512,2048]{1,0:T(8,128)S(1)} %get-tuple-element.55.refs_2_, ...), custom_call_target="tpu_custom_call" | custom-call | tf_op jit(solution)/shard_map/next3/pallas_call | solution.py:341
  80.4 0.2 collective-permute-start.7
  80.6 1.1 collective-permute-done.7.got_ref
  81.7 10.0 %all_to_all.49.refs_8_ = f32[32,8,128]{2,1,0:T(8,128)S(1)} all-to-all(f32[32,8,128]{2,1,0:T(8,128)S(1)} %spread.11), channel_id=1, replica_groups=mesh['row'=4,'col'=8] {'row','col'}, dimensions={0} | all-to-all | bytes 262144 | tf_op jit(solution)/shard_map/all_to_all | solution.py:324
  91.6 3.8 %next4.1 = (f32[128,128]{1,0:T(8,128)S(1)}, f32[128,128]{1,0:T(8,128)S(1)}, f32[8,128]{1,0:T(8,128)S(1)}, f32[8,128]{1,0:T(8,128)S(1)}, f32[8,128]{1,0:T(8,128)S(1)}) custom-call(f32[512,2048]{1,0:T(8,128)S(1)} %get-tuple-element.53.refs_0_, f32[512,2048]{1,0:T(8,128)S(1)} %get-tuple-element.54.refs_1_, f32[512,2048]{1,0:T(8,128)S(1)} %get-tuple-element.55.refs_2_, ...), custom_call_target="tpu_custom_call" | custom-call | tf_op jit(solution)/shard_map/next4/pallas_call | solution.py:341
  95.4 0.2 collective-permute-start.8
  95.6 1.1 collective-permute-done.8.got_ref
  96.7 10.0 %all_to_all.50.refs_8_ = f32[32,8,128]{2,1,0:T(8,128)S(1)} all-to-all(f32[32,8,128]{2,1,0:T(8,128)S(1)} %spread.12), channel_id=1, replica_groups=mesh['row'=4,'col'=8] {'row','col'}, dimensions={0} | all-to-all | bytes 262144 | tf_op jit(solution)/shard_map/all_to_all | solution.py:324
  106.6 3.8 %next5.1 = (f32[128,128]{1,0:T(8,128)S(1)}, f32[128,128]{1,0:T(8,128)S(1)}, f32[8,128]{1,0:T(8,128)S(1)}, f32[8,128]{1,0:T(8,128)S(1)}, f32[8,128]{1,0:T(8,128)S(1)}) custom-call(f32[512,2048]{1,0:T(8,128)S(1)} %get-tuple-element.53.refs_0_, f32[512,2048]{1,0:T(8,128)S(1)} %get-tuple-element.54.refs_1_, f32[512,2048]{1,0:T(8,128)S(1)} %get-tuple-element.55.refs_2_, ...), custom_call_target="tpu_custom_call" | custom-call | tf_op jit(solution)/shard_map/next5/pallas_call | solution.py:341
  110.4 0.2 collective-permute-start.9
  110.6 1.1 collective-permute-done.9.got_ref
  111.7 10.0 %all_to_all.51.refs_8_ = f32[32,8,128]{2,1,0:T(8,128)S(1)} all-to-all(f32[32,8,128]{2,1,0:T(8,128)S(1)} %spread.13), channel_id=1, replica_groups=mesh['row'=4,'col'=8] {'row','col'}, dimensions={0} | all-to-all | bytes 262144 | tf_op jit(solution)/shard_map/all_to_all | solution.py:324
  121.7 3.8 %next6.1 = (f32[128,128]{1,0:T(8,128)S(1)}, f32[128,128]{1,0:T(8,128)S(1)}, f32[8,128]{1,0:T(8,128)S(1)}, f32[8,128]{1,0:T(8,128)S(1)}, f32[8,128]{1,0:T(8,128)S(1)}) custom-call(f32[512,2048]{1,0:T(8,128)S(1)} %get-tuple-element.53.refs_0_, f32[512,2048]{1,0:T(8,128)S(1)} %get-tuple-element.54.refs_1_, f32[512,2048]{1,0:T(8,128)S(1)} %get-tuple-element.55.refs_2_, ...), custom_call_target="tpu_custom_call" | custom-call | tf_op jit(solution)/shard_map/next6/pallas_call | solution.py:341
  125.4 0.2 collective-permute-start.10
  125.6 1.1 collective-permute-done.10.got_ref
  126.7 10.0 %all_to_all.52.refs_8_ = f32[32,8,128]{2,1,0:T(8,128)S(1)} all-to-all(f32[32,8,128]{2,1,0:T(8,128)S(1)} %spread.14), channel_id=1, replica_groups=mesh['row'=4,'col'=8] {'row','col'}, dimensions={0} | all-to-all | bytes 262144 | tf_op jit(solution)/shard_map/all_to_all | solution.py:324
  136.7 3.8 %next7.1 = (f32[128,128]{1,0:T(8,128)S(1)}, f32[128,128]{1,0:T(8,128)S(1)}, f32[8,128]{1,0:T(8,128)S(1)}, f32[8,128]{1,0:T(8,128)S(1)}, f32[8,128]{1,0:T(8,128)S(1)}) custom-call(f32[512,2048]{1,0:T(8,128)S(1)} %get-tuple-element.53.refs_0_, f32[512,2048]{1,0:T(8,128)S(1)} %get-tuple-element.54.refs_1_, f32[512,2048]{1,0:T(8,128)S(1)} %get-tuple-element.55.refs_2_, ...), custom_call_target="tpu_custom_call" | custom-call | tf_op jit(solution)/shard_map/next7/pallas_call | solution.py:341
  140.5 0.2 collective-permute-start.11
  140.6 1.1 collective-permute-done.11.got_ref
  141.7 10.0 %all_to_all.53.refs_8_ = f32[32,8,128]{2,1,0:T(8,128)S(1)} all-to-all(f32[32,8,128]{2,1,0:T(8,128)S(1)} %spread.15), channel_id=1, replica_groups=mesh['row'=4,'col'=8] {'row','col'}, dimensions={0} | all-to-all | bytes 262144 | tf_op jit(solution)/shard_map/all_to_all | solution.py:324
  151.7 11.9 %last.1 = f32[4096,2048]{1,0:T(8,128)} custom-call(f32[512,2048]{1,0:T(8,128)S(1)} %get-tuple-element.53.refs_0_, f32[512,2048]{1,0:T(8,128)S(1)} %get-tuple-element.54.refs_1_, f32[512,2048]{1,0:T(8,128)S(1)} %get-tuple-element.55.refs_2_, f32[512,2048]{1,0:T(8,128)S(1)} %get-tuple-element.56.refs_3_, f32[512,2048]{1,0:T(8,128)S(1)} %get-tuple-element.57.refs_4_, ...), custom_call_target="tpu_custom_call" | custom-call | tf_op jit(solution)/shard_map/last/pallas_call | solution.py:356
  (9 shorter events, 0.1 us)
Async XLA Ops:
  0.8 10.4 %collective-permute-start.2 = (f32[8,512]{1,0:T(8,128)S(1)}, f32[8,512]{1,0:T(8,128)S(1)}, u32[]{:S(2)}, u32[]{:S(2)}) collective-permute-start(f32[8,512]{1,0:T(8,128)S(1)} %get-tuple-element.101), channel_id=1, source_target_pairs={{0,24},{1,25},{2,26},{3,27},{4,28},{5,29},{6,30},{7,31}} | collective-permute-start | bytes 49160 | tf_op jit(solution)/shard_map/ppermute | solution.py:277
  5.1 6.1 %collective-permute-start.1 = (f32[8,512]{1,0:T(8,128)S(1)}, f32[8,512]{1,0:T(8,128)S(1)}, u32[]{:S(2)}, u32[]{:S(2)}) collective-permute-start(f32[8,512]{1,0:T(8,128)S(1)} %get-tuple-element.102), channel_id=1, source_target_pairs={{0,16},{1,17},{2,18},{3,19},{4,20},{5,21},{6,22},{7,23}} | collective-permute-start | bytes 49160 | tf_op jit(solution)/shard_map/ppermute | solution.py:277
  6.4 4.8 %collective-permute-start = (f32[8,512]{1,0:T(8,128)S(1)}, f32[8,512]{1,0:T(8,128)S(1)}, u32[]{:S(2)}, u32[]{:S(2)}) collective-permute-start(f32[8,512]{1,0:T(8,128)S(1)} %get-tuple-element.103), channel_id=1, source_target_pairs={{0,8},{1,9},{2,10},{3,11},{4,12},{5,13},{6,14},{7,15}} | collective-permute-start | bytes 49160 | tf_op jit(solution)/shard_map/ppermute | solution.py:277
  25.5 3.5 %collective-permute-start.3 = (f32[16,8,512]{2,1,0:T(8,128)S(1)}, f32[16,8,512]{2,1,0:T(8,128)S(1)}, u32[]{:S(2)}, u32[]{:S(2)}) collective-permute-start(f32[16,8,512]{2,1,0:T(8,128)S(1)} %all_to_all.45.refs_0_.refs_4_), channel_id=1, source_target_pairs={{0,8},{8,0},{16,24},{24,16},{1,9},{9,1},{17,25},{25,17},{2,10},{10... | collective-permute-start | bytes 786440 | tf_op jit(solution)/shard_map/ppermute | solution.py:310
  35.4 1.4 collective-permute-start.4
  50.5 1.2 collective-permute-start.5
  65.4 1.2 collective-permute-start.6
  80.4 1.2 collective-permute-start.7
  95.4 1.2 collective-permute-start.8
  110.4 1.2 collective-permute-start.9
  125.4 1.2 collective-permute-start.10
  140.5 1.2 collective-permute-start.11
